TPU v7x, 128 devices: a whole 4x4x4 slice. The times are simulated.
128 devices in a mesh: lat: 32 (over z, x, core), lev: 4 (over y).
Axes of the slice: x: 4, y: 4, z: 4, core: 2. Of those that a mesh axis runs over, the one named last changes fastest.
Arguments:
- grid: bfloat16 [640, 128, 4, 1280], P('lat', 'lev'), may hold values from -6 to 6
- legendre: bfloat16 [640, 640, 640], P('lat'), may hold values from -0.25 to 0.25
- vertical: bfloat16 [128, 128], P('lev'), may hold values from -0.5 to 0.5
- damping: bfloat16 [128], P('lev'), may hold values from 1 to 16
- lon_counts: int32 [640], replicated, may hold values from 160 to 1280
- wave_slots: int32 [640], replicated, may hold values from 0 to 639, as said below
Outputs:
- filtered_grid: bfloat16 [640, 128, 4, 1280], P('lat', 'lev')
Inputs may be any that keep to these rules, and one draw needn't show every extreme that they name: wave_slots is a permutation; slot g * 5 + r holds a wavenumber from r * 128 to (r + 1) * 128 - 1.
All inputs are finite; a program needn't handle non-finite values.
Results may differ from a plain program's by a relative error of at most 0.0074.
Values may be sent and summed in bfloat16 or wider, within the bound.
A program may use at most 128 MiB of HBM per device.

v0:
```python
import functools
import math

import jax
import jax.numpy as jnp
from jax import lax
from jax.experimental import pallas as pl
from jax.experimental.pallas import tpu as pltpu
from jax.sharding import PartitionSpec as P

LAT, LEV = 32, 4
PEERS = LAT * LEV
ROUNDS = 5
ROWS = 20
LANES = 128
LONS = 1280
DEGREES = 640
BF16, F32 = jnp.bfloat16, jnp.float32
MESH = pl.DeviceIdType.MESH
NT = (((1,), (1,)), ((), ()))
TN = (((0,), (0,)), ((), ()))


def step_kernel(
    grid_ref, leg_ref, vd_ref, trig_ref, lon_ref, wave_ref,
    brecv, tab_out,
    gv, legv, tab, fsend, frecv, bsend, vdx, vfull, mixer, factor,
    pair32, half32, xr, legm, mixed,
    grid_sem, leg_sem, tab_sem, vsend_sem, vrecv_sem,
    fsend_sem, frecv_sem, bsend_sem, brecv_sem, own_sem,
):
    i = lax.axis_index("lat")
    j = lax.axis_index("lev")
    me = i * LEV + j
    z, x, c = i // 8, (i // 2) % 4, i % 2

    def partner(k):
        q = (k * 45) % PEERS
        dy, dc, dx, dz = q % 4, (q // 4) % 2, (q // 8) % 4, q // 32
        i2 = (((z + dz) % 4) * 4 + (x + dx) % 4) * 2 + (c + dc) % 2
        return i2, (j + dy) % LEV

    def grid_copy(a):
        return pltpu.make_async_copy(
            grid_ref.at[a].reshape(LANES, LONS), gv.at[a], grid_sem.at[a]
        )

    def leg_copy(r):
        return pltpu.make_async_copy(leg_ref.at[j * ROUNDS + r], legv.at[r], leg_sem.at[r])

    def start_grid(a, carry):
        grid_copy(a).start()
        return carry

    lax.fori_loop(0, ROWS, start_grid, 0)
    for r in range(ROUNDS):
        leg_copy(r).start()

    barrier = pltpu.get_barrier_semaphore()

    def greet(k, carry):
        pl.semaphore_signal(barrier, inc=1, device_id=partner(k), device_id_type=MESH)
        return carry

    lax.fori_loop(1, PEERS, greet, 0)

    def table(r):
        cb = trig_ref[0, r, :, 0:128]
        sb = trig_ref[1, r, :, 0:128]
        for q in range(LONS // 128):
            ca = trig_ref[0, r, :, 128 + q : 129 + q]
            sa = trig_ref[1, r, :, 128 + q : 129 + q]
            half32[pl.ds(0, 128, 2), :] = ca * cb - sa * sb
            half32[pl.ds(1, 128, 2), :] = -(sa * cb + ca * sb)
            tab[r, :, q * 128 : (q + 1) * 128] = half32[...].astype(BF16)
        pltpu.make_async_copy(tab.at[r], tab_out.at[r], tab_sem.at[r]).start()

    def forward(r):
        def pair(p, carry):
            if r == 0:
                grid_copy(2 * p).wait()
                grid_copy(2 * p + 1).wait()
            rows = gv.reshape(ROWS * LANES, LONS)[pl.ds(pl.multiple_of(p * 256, 256), 256), :]
            out = lax.dot_general(tab[r], rows, NT, preferred_element_type=F32).astype(BF16)
            fsend.at[r, 2 * p].reshape(256, 128)[...] = out[:, 0:128]
            fsend.at[r, 2 * p + 1].reshape(256, 128)[...] = out[:, 128:256]
            return carry

        lax.fori_loop(0, ROWS // 2, pair, 0)

    def send_forward(r):
        def send(k, carry):
            i2, j2 = partner(k)
            pltpu.make_async_remote_copy(
                src_ref=fsend.at[r, :, i2 * LEV + j2],
                dst_ref=frecv.at[r, j, pl.ds(i * ROWS, ROWS)],
                send_sem=fsend_sem.at[r],
                recv_sem=frecv_sem.at[r],
                device_id=(i2, j2),
                device_id_type=MESH,
            ).start()
            return carry

        lax.fori_loop(1, PEERS, send, 0)
        frecv[r, j, pl.ds(i * ROWS, ROWS)] = fsend[r, :, me]

    def send_back(r):
        def send(k, carry):
            i2, j2 = partner(k)
            pltpu.make_async_remote_copy(
                src_ref=bsend.at[r, j2, pl.ds(i2 * ROWS, ROWS)],
                dst_ref=brecv.at[r, :, me],
                send_sem=bsend_sem.at[r],
                recv_sem=brecv_sem.at[r],
                device_id=(i2, j2),
                device_id_type=MESH,
            ).start()
            return carry

        lax.fori_loop(1, PEERS, send, 0)
        pltpu.make_async_copy(
            bsend.at[r, j, pl.ds(i * ROWS, ROWS)], brecv.at[r, :, me], own_sem.at[r]
        ).start()

    def wait_bytes(ref, r, sem):
        most = ref.at[r].reshape(ROWS * PEERS, 2, LANES).at[pl.ds(0, ROWS * (PEERS - 1))]
        pltpu.make_async_copy(most, most, sem.at[r]).wait()

    def vertical_copy(d):
        return pltpu.make_async_remote_copy(
            src_ref=vd_ref,
            dst_ref=vdx.at[j],
            send_sem=vsend_sem,
            recv_sem=vrecv_sem,
            device_id=(i, (j + d) % LEV),
            device_id_type=MESH,
        )

    def build_mixer():
        three = vdx.at[pl.ds(0, LEV - 1)]
        pltpu.make_async_copy(three, three, vrecv_sem).wait()
        pltpu.make_async_copy(three, three, vsend_sem).wait()
        for p in range(LEV):
            vfull[p * 32 : (p + 1) * 32, :] = vdx[p, 0:32, :]
        row = lax.broadcasted_iota(jnp.int32, (512, 128), 0)
        col = lax.broadcasted_iota(jnp.int32, (512, 128), 1)
        pick = jnp.where(row // 4 == col, 1.0, 0.0).astype(BF16)
        tall = lax.dot_general(pick, vfull[...], NT, preferred_element_type=F32).astype(BF16)
        wide = lax.dot_general(tall, pick, NT, preferred_element_type=F32)
        row = lax.broadcasted_iota(jnp.int32, (512, 512), 0)
        col = lax.broadcasted_iota(jnp.int32, (512, 512), 1)
        mixer[...] = jnp.where(row % 4 == col % 4, wide, 0.0).astype(BF16)
        damp = vdx[0, 32:48, :].astype(F32)
        for p in range(1, LEV):
            damp = damp + vdx[p, 32:48, :].astype(F32)
        damp = lax.dot_general(damp.astype(BF16), pick, NT, preferred_element_type=F32)[0:1, :]
        for t in range(ROUNDS):
            n = (lax.broadcasted_iota(jnp.int32, (128, 512), 0) + 128 * t).astype(F32)
            ratio = n * (n + 1.0) / float(DEGREES * (DEGREES - 1))
            factor[t * 128 : (t + 1) * 128, :] = 1.0 / (1.0 + damp * (ratio * ratio))

    def spectral(r):
        wave = wave_ref[me * ROUNDS + r]
        weight = jnp.where(wave == 0, 1.0, 2.0).astype(F32)
        for p in range(LEV):
            pair32[...] = frecv.at[r, p].reshape(2 * DEGREES, 128)[...].astype(F32)
            for h in range(2):
                xr[:, h * 512 + p * 128 : h * 512 + (p + 1) * 128] = pair32[
                    pl.ds(h, DEGREES, 2), :
                ].astype(BF16)
        keep = jnp.where(2 * wave < lon_ref[...], 1.0, 0.0)
        for t in range(r, ROUNDS):
            n = lax.broadcasted_iota(jnp.int32, (128, DEGREES), 0) + 128 * t
            tile = jnp.where(n >= wave, legv[r, t * 128 : (t + 1) * 128, :].astype(F32), 0.0)
            tile = (tile * keep).astype(BF16)
            legm[t * 128 : (t + 1) * 128, :] = tile
            spec = jnp.dot(tile, xr[...], preferred_element_type=F32).astype(BF16)
            for h in range(2):
                part = spec[:, h * 512 : (h + 1) * 512]
                total = part.astype(F32) + jnp.dot(
                    part, mixer[...], preferred_element_type=F32
                )
                total = total * factor[t * 128 : (t + 1) * 128, :] * weight
                mixed[t * 128 : (t + 1) * 128, h * 512 : (h + 1) * 512] = total.astype(BF16)
        for s in range(ROUNDS):
            out = lax.dot_general(
                legm[r * 128 :, s * 128 : (s + 1) * 128],
                mixed[r * 128 :, :],
                TN,
                preferred_element_type=F32,
            )
            for p in range(LEV):
                for h in range(2):
                    half32[pl.ds(h, 128, 2), :] = out[
                        :, h * 512 + p * 128 : h * 512 + (p + 1) * 128
                    ]
                bsend.at[r, p].reshape(2 * DEGREES, 128)[s * 256 : (s + 1) * 256, :] = half32[
                    ...
                ].astype(BF16)

    table(0)
    forward(0)
    pl.semaphore_wait(barrier, PEERS - 1)
    send_forward(0)
    for d in range(1, LEV):
        vertical_copy(d).start()
    vdx[j] = vd_ref[...]
    for r in range(1, ROUNDS):
        table(r)
        forward(r)
        send_forward(r)
    build_mixer()
    for r in range(ROUNDS):
        leg_copy(r).wait()
        wait_bytes(frecv, r, frecv_sem)
        spectral(r)
        send_back(r)
    for r in range(ROUNDS):
        pltpu.make_async_copy(tab.at[r], tab_out.at[r], tab_sem.at[r]).wait()
        wait_bytes(fsend, r, fsend_sem)
        wait_bytes(bsend, r, bsend_sem)
        pltpu.make_async_copy(
            bsend.at[r, j, pl.ds(i * ROWS, ROWS)], brecv.at[r, :, me], own_sem.at[r]
        ).wait()
        wait_bytes(brecv, r, brecv_sem)


def step(grid, legendre, vd, trig, lon, waves):
    dma = pltpu.SemaphoreType.DMA
    vmem = pl.BlockSpec(memory_space=pltpu.VMEM)
    any_spec = pl.BlockSpec(memory_space=pl.ANY)
    return pl.pallas_call(
        step_kernel,
        out_shape=(
            jax.ShapeDtypeStruct((ROUNDS, ROWS, PEERS, 2, LANES), BF16),
            jax.ShapeDtypeStruct((ROUNDS, 256, LONS), BF16),
        ),
        in_specs=[any_spec, any_spec, vmem, vmem, vmem, pl.BlockSpec(memory_space=pltpu.SMEM)],
        out_specs=(any_spec, any_spec),
        scratch_shapes=[
            pltpu.VMEM((ROWS, LANES, LONS), BF16),
            pltpu.VMEM((ROUNDS, DEGREES, DEGREES), BF16),
            pltpu.VMEM((ROUNDS, 256, LONS), BF16),
            pltpu.VMEM((ROUNDS, ROWS, PEERS, 2, LANES), BF16),
            pltpu.VMEM((ROUNDS, LEV, DEGREES, 2, LANES), BF16),
            pltpu.VMEM((ROUNDS, LEV, DEGREES, 2, LANES), BF16),
            pltpu.VMEM((LEV, 48, 128), BF16),
            pltpu.VMEM((128, 128), BF16),
            pltpu.VMEM((512, 512), BF16),
            pltpu.VMEM((DEGREES, 512), F32),
            pltpu.VMEM((2 * DEGREES, 128), F32),
            pltpu.VMEM((256, 128), F32),
            pltpu.VMEM((DEGREES, 1024), BF16),
            pltpu.VMEM((DEGREES, DEGREES), BF16),
            pltpu.VMEM((DEGREES, 1024), BF16),
            dma((ROWS,)), dma((ROUNDS,)), dma((ROUNDS,)), dma, dma,
            dma((ROUNDS,)), dma((ROUNDS,)), dma((ROUNDS,)), dma((ROUNDS,)), dma((ROUNDS,)),
        ],
        compiler_params=pltpu.CompilerParams(
            collective_id=0, has_side_effects=True, vmem_limit_bytes=62 * 2**20
        ),
    )(grid, legendre, vd, trig, lon, waves)


CHUNK = 4


def inverse_kernel(back_ref, tab_ref, out_ref, lhs):
    for a in range(CHUNK):
        for r in range(ROUNDS):
            block = back_ref.at[r, a].reshape(256, 128)[...]
            lhs[a * 128 : (a + 1) * 128, r * 256 : (r + 1) * 256] = block.T
    out = jnp.dot(lhs[...], tab_ref[...], preferred_element_type=F32).astype(BF16)
    out_ref[...] = out.reshape(CHUNK, 32, 4, LONS)


def inverse(back, tab):
    return pl.pallas_call(
        inverse_kernel,
        grid=(ROWS // CHUNK,),
        out_shape=jax.ShapeDtypeStruct((ROWS, 32, 4, LONS), BF16),
        in_specs=[
            pl.BlockSpec((ROUNDS, CHUNK, PEERS, 2, LANES), lambda s: (0, s, 0, 0, 0)),
            pl.BlockSpec((LONS, LONS), lambda s: (0, 0)),
        ],
        out_specs=pl.BlockSpec((CHUNK, 32, 4, LONS), lambda s: (s, 0, 0, 0)),
        scratch_shapes=[pltpu.VMEM((CHUNK * 128, LONS), BF16)],
        compiler_params=pltpu.CompilerParams(vmem_limit_bytes=40 * 2**20),
    )(back, tab)


def per_device(grid, legendre, vertical, damping, lon_counts, wave_slots):
    points = jnp.arange(256, dtype=jnp.int32)
    points = jnp.where(points < 128, points, (points - 128) * 128 % LONS)
    waves = wave_slots.reshape(PEERS, ROUNDS).T
    phase = (waves[:, :, None] * points % LONS).astype(F32) * (2.0 * math.pi / LONS)
    scale = jnp.where(jnp.arange(256) < 128, 1.0 / math.sqrt(LONS), 1.0)
    trig = jnp.stack([jnp.cos(phase) * scale, jnp.sin(phase) * scale])
    row = lax.dynamic_update_slice_in_dim(
        jnp.zeros((128,), BF16), damping, lax.axis_index("lev") * 32, 0
    )
    vd = jnp.concatenate([vertical, jnp.broadcast_to(row, (16, 128))])
    back, tab = step(grid, legendre, vd, trig, lon_counts.reshape(1, DEGREES), wave_slots)
    return inverse(back, tab.reshape(LONS, LONS))


def solution(mesh):
    return jax.shard_map(
        per_device,
        mesh=mesh,
        in_specs=(
            P("lat", "lev", None, None),
            P("lat", None, None),
            P("lev", None),
            P("lev"),
            P(),
            P(),
        ),
        out_specs=P("lat", "lev", None, None),
        check_vma=False,
    )
```

profile of v0, /device:TPU:1, one launch (start us, length us, event | category | flops | bytes accessed | tf_op | source)
XLA Modules:
  0.0 188.7 jit_solution(7219284921176604217)
XLA Ops:
  0.0 0.8 dynamic_update_slice.3
  0.9 1.3 reshape.71.lon_ref
  2.2 1.3 pad_maximum_fusion.1.vd_ref
  3.4 0.9 reshape.70
  4.3 0.1 copy.7
  4.4 2.8 %cosine_multiply_fusion = (f32[1,5,128,256]{3,2,1,0:T(8,128)S(1)}, f32[1,5,128,256]{3,2,1,0:T(8,128)S(1)}) fusion(f32[256]{0:T(256)S(1)} %compare_select_fusion, s32[256]{0:T(256)S(1)} %compare_select_fusion.1, s32[5,128]{1,0:T(8,128)S(1)} %copy.7), kind=kLoop, calls=%fused_computation.5 | loop fusion | flops 1802240 | bytes 1315328 | tf_op jit(solution)/shard_map/mul | solution.py:298
  7.2 1.2 pad_maximum_fusion.trig_ref
  8.4 162.8 %shard_map.64 = (bf16[5,20,128,2,128]{4,3,2,1,0:T(2,128)(2,1)}, bf16[5,256,1280]{2,1,0:T(8,128)(2,1)}) custom-call(bf16[20,32,4,1280]{3,2,1,0:T(4,128)(2,1)} %grid_ref.1, bf16[20,640,640]{2,1,0:T(8,128)(2,1)} %leg_ref.1, bf16[48,128]{1,0:T(8,128)(2,1)} %pad_maximum_fusion.1.vd_ref, f32[2,5,128,256]{3,2,1,0:T(8,128)} %pad_maximum_fusion.trig_ref, ...), custom_call_target="tpu_custom_call" | custom-call | tf_op jit(solution)/shard_map/pallas_call | solution.py:232
  171.2 0.0 copy-start
  171.2 2.9 %copy-done = bf16[5,20,128,2,128]{4,3,2,1,0:T(2,128)(2,1)S(1)} copy-done((bf16[5,20,128,2,128]{4,3,2,1,0:T(2,128)(2,1)S(1)}, bf16[5,20,128,2,128]{4,3,2,1,0:T(2,128)(2,1)}, u32[]{:S(2)}) %copy-start) | copy-done | bytes 6553624
  174.1 0.0 copy-start.1
  174.1 1.9 %copy-done.1 = bf16[5,256,1280]{2,1,0:T(8,128)(2,1)S(1)} copy-done((bf16[5,256,1280]{2,1,0:T(8,128)(2,1)S(1)}, bf16[5,256,1280]{2,1,0:T(8,128)(2,1)}, u32[]{:S(2)}) %copy-start.1) | copy-done | bytes 3276824
  176.0 12.7 %shard_map.65 = bf16[20,32,4,1280]{3,2,1,0:T(4,128)(2,1)} custom-call(bf16[5,20,128,2,128]{4,3,2,1,0:T(2,128)(2,1)S(1)} %copy-done, bf16[1280,1280]{1,0:T(8,128)(2,1)S(1)} %bitcast.2), custom_call_target="tpu_custom_call" | custom-call | tf_op jit(solution)/shard_map/pallas_call | solution.py:278
  (4 shorter events, 0.0 us)
Async XLA Ops:
  171.2 2.9 %copy-start = (bf16[5,20,128,2,128]{4,3,2,1,0:T(2,128)(2,1)S(1)}, bf16[5,20,128,2,128]{4,3,2,1,0:T(2,128)(2,1)}, u32[]{:S(2)}) copy-start(bf16[5,20,128,2,128]{4,3,2,1,0:T(2,128)(2,1)} %get-tuple-element.7.back_ref) | copy-start | bytes 19660804
  174.1 1.9 %copy-start.1 = (bf16[5,256,1280]{2,1,0:T(8,128)(2,1)S(1)}, bf16[5,256,1280]{2,1,0:T(8,128)(2,1)}, u32[]{:S(2)}) copy-start(bf16[5,256,1280]{2,1,0:T(8,128)(2,1)} %get-tuple-element.8) | copy-start | bytes 9830404
where the time goes:
time: 189 us
  Pallas kernels  176 us (93%)
  local copies, waits for them, and re-layouts  7.84 us (4%)
  other arithmetic  5.29 us (3%)
    pallas_call x1, Pallas kernels, step(): pl.pallas_call(step_kernel, out_shape=(jax.ShapeDtypeStruct((ROUNDS, ROWS...  163 us
    pallas_call x1, Pallas kernels, inverse(): pl.pallas_call(inverse_kernel, grid=(ROWS // CHUNK,), out_shape=jax.Shape...  12.7 us
    unnamed x4, local copies, waits for them, and re-layouts  4.78 us

commit v1 on v0

v1 whole, which is shorter than its diff:
```python
import functools
import math

import jax
import jax.numpy as jnp
from jax import lax
from jax.experimental import pallas as pl
from jax.experimental.pallas import tpu as pltpu
from jax.sharding import PartitionSpec as P

LAT, LEV = 32, 4
PEERS = LAT * LEV
ROUNDS = 5
ROWS = 20
LANES = 128
LONS = 1280
DEGREES = 640
BF16, F32 = jnp.bfloat16, jnp.float32
CHUNK = 4
PIECE = 10
MESH = pl.DeviceIdType.MESH
NT = (((1,), (1,)), ((), ()))
TN = (((0,), (0,)), ((), ()))


def step_kernel(
    grid_ref, leg_ref, vert_ref, damp_ref, lon_ref, wave_ref,
    last, part_out, tab_out,
    gv, legv, tab, fsend, frecv, bsend, brecv, vertx, dampx, damp16, vfull, mixer, factor,
    wave32, trig, pair32, half32, xr, legm, mixed, lhs, part,
    grid_sem, leg_sem, tab_sem, vsend_sem, vrecv_sem,
    fsend_sem, frecv_sem, bsend_sem, brecv_sem, own_sem, part_sem,
):
    i = lax.axis_index("lat")
    j = lax.axis_index("lev")
    me = i * LEV + j
    z, x, c = i // 8, (i // 2) % 4, i % 2

    far_z = [(z + d) % 4 * 8 for d in range(4)]
    far_x = [(x + d) % 4 * 2 for d in range(4)]
    far_c = [c, (c + 1) % 2]
    far_y = [(j + d) % LEV for d in range(LEV)]

    def to_partners(act):
        for u in range(1, 8):
            q = 45 * u % PEERS
            act(far_z[q // 32] + far_x[q // 8 % 4] + far_c[q // 4 % 2], far_y[q % 4])

        def plane(t, carry):
            for u in range(8):
                q = 45 * u % 8
                high = 13 * t + 45 * u // 8
                base = lax.rem(z + lax.div(high, 4), 4) * 8 + lax.rem(x + high, 4) * 2
                act(base + far_c[q // 4], far_y[q % 4])
            return carry

        lax.fori_loop(1, 16, plane, 0)

    def grid_copy(a):
        return pltpu.make_async_copy(
            grid_ref.at[pl.ds(a * CHUNK, CHUNK)].reshape(CHUNK * LANES, LONS),
            gv.at[a],
            grid_sem.at[a],
        )

    def leg_copy(r):
        return pltpu.make_async_copy(leg_ref.at[j * ROUNDS + r], legv.at[r], leg_sem.at[r])

    def tab_copy():
        return pltpu.make_async_copy(tab.at[ROUNDS - 1], tab_out, tab_sem)

    def landing(r):
        return brecv.at[r] if r < ROUNDS - 1 else last

    for a in range(ROWS // CHUNK):
        grid_copy(a).start()
    barrier = pltpu.get_barrier_semaphore()
    for k in range(1, PEERS):
        q = (k * 45) % PEERS
        pl.semaphore_signal(
            barrier,
            inc=1,
            device_id=(far_z[q // 32] + far_x[q // 8 % 4] + far_c[q // 4 % 2], far_y[q % 4]),
            device_id_type=MESH,
        )
    for r in range(ROUNDS):
        leg_copy(r).start()
    damp16[...] = jnp.zeros_like(damp16)
    damp16[:, 0:32] = jnp.broadcast_to(damp_ref[...].astype(F32).reshape(1, 32), (16, 32)).astype(
        BF16
    )

    def table(r):
        def spread(g, carry):
            wave32[pl.ds(g, 1), :] = jnp.full((1, 128), wave_ref[g * ROUNDS + r], jnp.int32)
            return carry

        lax.fori_loop(0, PEERS, spread, 0, unroll=8)
        wave = wave32[...].astype(F32)
        lane = lax.broadcasted_iota(jnp.int32, (PEERS, 128), 1).astype(F32)
        scale = 1.0 / math.sqrt(LONS)
        cb, sb = unit_circle(wave * lane)
        cb, sb = cb * scale, sb * scale
        trig[0], trig[1] = unit_circle(wave * lane * 128.0)
        for q in range(LONS // 128):
            ca = trig[0, :, q : q + 1]
            sa = trig[1, :, q : q + 1]
            half32[pl.ds(0, 128, 2), :] = ca * cb - sa * sb
            half32[pl.ds(1, 128, 2), :] = -(sa * cb + ca * sb)
            tab[r, :, q * 128 : (q + 1) * 128] = half32[...].astype(BF16)
        if r == ROUNDS - 1:
            tab_copy().start()

    def forward(r, first, count):
        def pair(p, carry):
            if r == 0:

                @pl.when(p % 2 == 0)
                def _():
                    grid_copy(p // 2).wait()

            rows = gv.reshape(ROWS * LANES, LONS)[pl.ds(pl.multiple_of(p * 256, 256), 256), :]
            out = lax.dot_general(tab[r], rows, NT, preferred_element_type=F32).astype(BF16)
            fsend.at[r, 2 * p].reshape(256, 128)[...] = out[:, 0:128]
            fsend.at[r, 2 * p + 1].reshape(256, 128)[...] = out[:, 128:256]
            return carry

        lax.fori_loop(first // 2, (first + count) // 2, pair, 0)

    def send_forward(r, first, count):
        def send(i2, j2):
            pltpu.make_async_remote_copy(
                src_ref=fsend.at[r, pl.ds(first, count), i2 * LEV + j2],
                dst_ref=frecv.at[r, j, pl.ds(i * ROWS + first, count)],
                send_sem=fsend_sem.at[r],
                recv_sem=frecv_sem.at[r],
                device_id=(i2, j2),
                device_id_type=MESH,
            ).start()

        to_partners(send)
        frecv[r, j, pl.ds(i * ROWS + first, count)] = fsend[r, first : first + count, me]

    def send_back(r):
        def send(i2, j2):
            pltpu.make_async_remote_copy(
                src_ref=bsend.at[r, j2, pl.ds(i2 * ROWS, ROWS)],
                dst_ref=landing(r).at[:, me],
                send_sem=bsend_sem.at[r],
                recv_sem=brecv_sem.at[r],
                device_id=(i2, j2),
                device_id_type=MESH,
            ).start()

        to_partners(send)
        if r < ROUNDS - 1:
            brecv[r, :, me] = bsend[r, j, pl.ds(i * ROWS, ROWS)]
        else:
            own_copy().start()

    def own_copy():
        return pltpu.make_async_copy(
            bsend.at[ROUNDS - 1, j, pl.ds(i * ROWS, ROWS)], last.at[:, me], own_sem
        )

    def part_copy(s):
        return pltpu.make_async_copy(
            part.at[s % 2], part_out.at[pl.ds(s * CHUNK * 128, CHUNK * 128)], part_sem.at[s % 2]
        )

    def wait_bytes(ref, r, sem):
        most = ref.reshape(ROWS * PEERS, 2, LANES).at[pl.ds(0, ROWS * (PEERS - 1))]
        pltpu.make_async_copy(most, most, sem.at[r]).wait()

    def level_copy(src, dst, s, d):
        return pltpu.make_async_remote_copy(
            src_ref=src,
            dst_ref=dst.at[j],
            send_sem=vsend_sem.at[s],
            recv_sem=vrecv_sem.at[s],
            device_id=(i, (j + d) % LEV),
            device_id_type=MESH,
        )

    def build_mixer():
        for s, ref in enumerate((vertx, dampx)):
            three = ref.at[pl.ds(0, LEV - 1)]
            pltpu.make_async_copy(three, three, vrecv_sem.at[s]).wait()
            pltpu.make_async_copy(three, three, vsend_sem.at[s]).wait()
        for p in range(LEV):
            vfull[p * 32 : (p + 1) * 32, :] = vertx[p]
        row = lax.broadcasted_iota(jnp.int32, (512, 128), 0)
        col = lax.broadcasted_iota(jnp.int32, (512, 128), 1)
        pick = jnp.where(row // 4 == col, 1.0, 0.0).astype(BF16)
        tall = lax.dot_general(pick, vfull[...], NT, preferred_element_type=F32).astype(BF16)
        wide = lax.dot_general(tall, pick, NT, preferred_element_type=F32)
        row = lax.broadcasted_iota(jnp.int32, (512, 512), 0)
        col = lax.broadcasted_iota(jnp.int32, (512, 512), 1)
        mixer[...] = jnp.where(row % 4 == col % 4, wide, 0.0).astype(BF16)
        near = jnp.where(row[:, 0:128] // 4 % 32 == col[:, 0:128], 1.0, 0.0).astype(BF16)
        lane = lax.broadcasted_iota(jnp.int32, (16, 512), 1)
        damp = jnp.zeros((16, 512), F32)
        for p in range(LEV):
            found = lax.dot_general(dampx[p], near, NT, preferred_element_type=F32)
            damp = damp + jnp.where(lane // 128 == p, found, 0.0)
        damp = damp[0:1, :]
        for t in range(ROUNDS):
            n = (lax.broadcasted_iota(jnp.int32, (128, 512), 0) + 128 * t).astype(F32)
            ratio = n * (n + 1.0) / float(DEGREES * (DEGREES - 1))
            factor[t * 128 : (t + 1) * 128, :] = 1.0 / (1.0 + damp * (ratio * ratio))

    def spectral(r):
        wave = wave_ref[me * ROUNDS + r]
        weight = jnp.where(wave == 0, 1.0, 2.0).astype(F32)
        for p in range(LEV):
            pair32[...] = frecv.at[r, p].reshape(2 * DEGREES, 128)[...].astype(F32)
            for h in range(2):
                xr[:, h * 512 + p * 128 : h * 512 + (p + 1) * 128] = pair32[
                    pl.ds(h, DEGREES, 2), :
                ].astype(BF16)
        keep = jnp.where(2 * wave < lon_ref[...], 1.0, 0.0).reshape(1, DEGREES)
        for t in range(r, ROUNDS):
            n = lax.broadcasted_iota(jnp.int32, (128, DEGREES), 0) + 128 * t
            tile = jnp.where(n >= wave, legv[r, t * 128 : (t + 1) * 128, :].astype(F32), 0.0)
            tile = (tile * keep).astype(BF16)
            legm[t * 128 : (t + 1) * 128, :] = tile
            spec = jnp.dot(tile, xr[...], preferred_element_type=F32).astype(BF16)
            for h in range(2):
                part = spec[:, h * 512 : (h + 1) * 512]
                total = part.astype(F32) + jnp.dot(
                    part, mixer[...], preferred_element_type=F32
                )
                total = total * factor[t * 128 : (t + 1) * 128, :] * weight
                mixed[t * 128 : (t + 1) * 128, h * 512 : (h + 1) * 512] = total.astype(BF16)
        for s in range(ROUNDS):
            out = lax.dot_general(
                legm[r * 128 :, s * 128 : (s + 1) * 128],
                mixed[r * 128 :, :],
                TN,
                preferred_element_type=F32,
            )
            for p in range(LEV):
                for h in range(2):
                    half32[pl.ds(h, 128, 2), :] = out[
                        :, h * 512 + p * 128 : h * 512 + (p + 1) * 128
                    ]
                bsend.at[r, p].reshape(2 * DEGREES, 128)[s * 256 : (s + 1) * 256, :] = half32[
                    ...
                ].astype(BF16)

    table(0)
    forward(0, 0, 12)
    pl.semaphore_wait(barrier, PEERS - 1)
    send_forward(0, 0, 12)
    forward(0, 12, 8)
    send_forward(0, 12, 8)
    for d in range(1, LEV):
        level_copy(vert_ref, vertx, 0, d).start()
        level_copy(damp16, dampx, 1, d).start()
    vertx[j] = vert_ref[...]
    dampx[j] = damp16[...]
    for r in range(1, ROUNDS):
        table(r)
        forward(r, 0, ROWS)
        send_forward(r, 0, ROWS)
    build_mixer()
    for r in range(ROUNDS):
        leg_copy(r).wait()
        wait_bytes(frecv.at[r], r, frecv_sem)
        spectral(r)
        send_back(r)
    for r in range(ROUNDS - 1):
        wait_bytes(brecv.at[r], r, brecv_sem)
    for s in range(ROWS // CHUNK):
        for a in range(CHUNK):
            for r in range(ROUNDS - 1):
                block = brecv.at[r, s * CHUNK + a].reshape(256, 128)[...]
                lhs[a * 128 : (a + 1) * 128, r * 256 : (r + 1) * 256] = block.T
        if s >= 2:
            part_copy(s - 2).wait()
        part[s % 2] = jnp.dot(
            lhs[...],
            tab[0 : ROUNDS - 1].reshape((ROUNDS - 1) * 256, LONS),
            preferred_element_type=F32,
        ).astype(BF16)
        part_copy(s).start()
    for s in range(ROWS // CHUNK - 2, ROWS // CHUNK):
        part_copy(s).wait()
    tab_copy().wait()
    for r in range(ROUNDS):
        wait_bytes(fsend.at[r], r, fsend_sem)
        wait_bytes(bsend.at[r], r, bsend_sem)
    own_copy().wait()
    wait_bytes(last, ROUNDS - 1, brecv_sem)


def unit_circle(steps):
    turns = jnp.floor(steps * (1.0 / LONS))
    rest = steps - turns * LONS
    rest = jnp.where(rest < 0.0, rest + LONS, rest)
    rest = jnp.where(rest >= LONS, rest - LONS, rest)
    quarter = jnp.floor(rest * (4.0 / LONS) + 0.5)
    y = (rest - quarter * (LONS // 4)) * (2.0 * math.pi / LONS)
    y2 = y * y
    sine = y * (1 + y2 * (-1 / 6 + y2 * (1 / 120 + y2 * (-1 / 5040 + y2 * (1 / 362880)))))
    cosine = 1 + y2 * (
        -1 / 2 + y2 * (1 / 24 + y2 * (-1 / 720 + y2 * (1 / 40320 - y2 * (1 / 3628800))))
    )
    odd = (quarter == 1.0) | (quarter == 3.0)
    first = jnp.where(odd, sine, cosine)
    second = jnp.where(odd, cosine, sine)
    back = (quarter == 2.0) | (quarter == 3.0)
    left = (quarter == 1.0) | (quarter == 2.0)
    return jnp.where(left, -first, first), jnp.where(back, -second, second)


def step(grid, legendre, vertical, damp, lon, waves):
    dma = pltpu.SemaphoreType.DMA
    vmem = pl.BlockSpec(memory_space=pltpu.VMEM)
    any_spec = pl.BlockSpec(memory_space=pl.ANY)
    return pl.pallas_call(
        step_kernel,
        out_shape=(
            jax.ShapeDtypeStruct((ROWS, PEERS, 2, LANES), BF16),
            jax.ShapeDtypeStruct((ROWS * LANES, LONS), BF16),
            jax.ShapeDtypeStruct((256, LONS), BF16),
        ),
        in_specs=[any_spec, any_spec, vmem, vmem, vmem, pl.BlockSpec(memory_space=pltpu.SMEM)],
        out_specs=(any_spec, any_spec, any_spec),
        scratch_shapes=[
            pltpu.VMEM((ROWS // CHUNK, CHUNK * LANES, LONS), BF16),
            pltpu.VMEM((ROUNDS, DEGREES, DEGREES), BF16),
            pltpu.VMEM((ROUNDS, 256, LONS), BF16),
            pltpu.VMEM((ROUNDS, ROWS, PEERS, 2, LANES), BF16),
            pltpu.VMEM((ROUNDS, LEV, DEGREES, 2, LANES), BF16),
            pltpu.VMEM((ROUNDS, LEV, DEGREES, 2, LANES), BF16),
            pltpu.VMEM((ROUNDS - 1, ROWS, PEERS, 2, LANES), BF16),
            pltpu.VMEM((LEV, 32, 128), BF16),
            pltpu.VMEM((LEV, 16, 128), BF16),
            pltpu.VMEM((16, 128), BF16),
            pltpu.VMEM((128, 128), BF16),
            pltpu.VMEM((512, 512), BF16),
            pltpu.VMEM((DEGREES, 512), F32),
            pltpu.VMEM((PEERS, 128), jnp.int32),
            pltpu.VMEM((2, PEERS, 128), F32),
            pltpu.VMEM((2 * DEGREES, 128), F32),
            pltpu.VMEM((256, 128), F32),
            pltpu.VMEM((DEGREES, 1024), BF16),
            pltpu.VMEM((DEGREES, DEGREES), BF16),
            pltpu.VMEM((DEGREES, 1024), BF16),
            pltpu.VMEM((CHUNK * 128, (ROUNDS - 1) * 256), BF16),
            pltpu.VMEM((2, CHUNK * 128, LONS), BF16),
            dma((ROWS // CHUNK,)), dma((ROUNDS,)), dma, dma((2,)), dma((2,)),
            dma((ROUNDS,)), dma((ROUNDS,)), dma((ROUNDS,)), dma((ROUNDS,)), dma, dma((2,)),
        ],
        compiler_params=pltpu.CompilerParams(
            collective_id=0, has_side_effects=True, vmem_limit_bytes=62 * 2**20
        ),
    )(grid, legendre, vertical, damp, lon, waves)


def finish_kernel(last_ref, tab_ref, part_ref, out_ref, lhs, stage, sem):
    s = pl.program_id(0)
    slot = s % 2

    def out_copy(step, where):
        return pltpu.make_async_copy(
            stage.at[where],
            out_ref.at[pl.ds(step * PIECE, PIECE)].reshape(PIECE * LANES, LONS),
            sem.at[where],
        )

    for a in range(PIECE):
        lhs[a * 128 : (a + 1) * 128, :] = last_ref.at[a].reshape(256, 128)[...].T

    @pl.when(s >= 2)
    def _():
        out_copy(s - 2, slot).wait()

    out = jnp.dot(lhs[...], tab_ref[...], preferred_element_type=F32)
    stage[slot] = (out + part_ref[...].astype(F32)).astype(BF16)
    out_copy(s, slot).start()

    @pl.when(s == pl.num_programs(0) - 1)
    def _():
        out_copy(s - 1, 1 - slot).wait()
        out_copy(s, slot).wait()


def finish(last, part, tab):
    return pl.pallas_call(
        finish_kernel,
        grid=(ROWS // PIECE,),
        out_shape=jax.ShapeDtypeStruct((ROWS, 32, 4, LONS), BF16),
        in_specs=[
            pl.BlockSpec((PIECE, PEERS, 2, LANES), lambda s: (s, 0, 0, 0)),
            pl.BlockSpec((256, LONS), lambda s: (0, 0)),
            pl.BlockSpec((PIECE * 128, LONS), lambda s: (s, 0)),
        ],
        out_specs=pl.BlockSpec(memory_space=pl.ANY),
        scratch_shapes=[
            pltpu.VMEM((PIECE * 128, 256), BF16),
            pltpu.VMEM((2, PIECE * 128, LONS), BF16),
            pltpu.SemaphoreType.DMA((2,)),
        ],
        compiler_params=pltpu.CompilerParams(vmem_limit_bytes=62 * 2**20),
    )(last, tab, part)


def per_device(grid, legendre, vertical, damping, lon_counts, wave_slots):
    last, part, tab = step(grid, legendre, vertical, damping, lon_counts, wave_slots)
    return finish(last, part, tab)


def solution(mesh):
    return jax.shard_map(
        per_device,
        mesh=mesh,
        in_specs=(
            P("lat", "lev", None, None),
            P("lat", None, None),
            P("lev", None),
            P("lev"),
            P(),
            P(),
        ),
        out_specs=P("lat", "lev", None, None),
        check_vma=False,
    )
```

time: 189 us -> 163 us (0.86)
  Pallas kernels: 176 us -> 163 us
  local copies, waits for them, and re-layouts: 7.84 us -> 0 us
  other arithmetic: 5.29 us -> 0 us
    pallas_call x2, Pallas kernels: 176 us -> 163 us  [the longest x1 156 us: step(): pl.pallas_call(step_kernel, out_shape=(jax.ShapeDtypeStruct((ROWS, PEERS,...]
    unnamed x4 -> x0, local copies, waits for them, and re-layouts: 4.78 us -> none
    mul x1 -> x0, other arithmetic: 2.78 us -> none  [per_device(): trig = jnp.stack([jnp.cos(phase) * scale, jnp.sin(phase) * scale])]
    reshape x2 -> x0, local copies, waits for them, and re-layouts: 2.16 us -> none  [the longest x1 1.28 us: per_device(): lon_counts.reshape(1, DEGREES)]
where the time goes in v1:
time: 163 us
  Pallas kernels  163 us (100%)
    pallas_call x1, Pallas kernels, step(): pl.pallas_call(step_kernel, out_shape=(jax.ShapeDtypeStruct((ROWS, PEERS,...  156 us
    pallas_call x1, Pallas kernels, finish(): pl.pallas_call(finish_kernel, grid=(ROWS // PIECE,), out_shape=jax.ShapeD...  6.77 us

profile of v1, /device:TPU:1, one launch (start us, length us, event | category | flops | bytes accessed | tf_op | source)
XLA Modules:
  0.0 163.1 jit_solution(11422689393378124888)
XLA Ops:
  0.0 156.1 %shard_map.64 = (bf16[20,128,2,128]{3,2,1,0:T(2,128)(2,1)}, bf16[2560,1280]{1,0:T(8,128)(2,1)}, bf16[256,1280]{1,0:T(8,128)(2,1)}) custom-call(bf16[20,32,4,1280]{3,2,1,0:T(4,128)(2,1)} %grid_ref.1, bf16[20,640,640]{2,1,0:T(8,128)(2,1)} %leg_ref.1, bf16[32,128]{1,0:T(8,128)(2,1)} %vert_ref.1, bf16[32]{0:T(256)(128)(2,1)} %damp_ref.1, s32[640]{0:T(1024)} %lon_ref.1, ...), custom_call_target="tpu_custom_call" | custom-call | tf_op jit(solution)/shard_map/pallas_call | solution.py:321
  156.1 6.8 %shard_map.65 = bf16[20,32,4,1280]{3,2,1,0:T(4,128)(2,1)} custom-call(bf16[20,128,2,128]{3,2,1,0:T(2,128)(2,1)} %get-tuple-element.8.last_ref, bf16[256,1280]{1,0:T(8,128)(2,1)} %get-tuple-element.9.tab_ref, bf16[2560,1280]{1,0:T(8,128)(2,1)} %get-tuple-element.10.part_ref), custom_call_target="tpu_custom_call" | custom-call | tf_op jit(solution)/shard_map/pallas_call | solution.py:391

commit v2 on v1

--- a/solution.py
+++ b/solution.py
@@ -24,12 +24,12 @@
 
 
 def step_kernel(
-    grid_ref, leg_ref, vert_ref, damp_ref, lon_ref, wave_ref,
+    grid_ref, leg_ref, vert_ref, damp_hbm, lon_hbm, wave_hbm,
     last, part_out, tab_out,
-    gv, legv, tab, fsend, frecv, bsend, brecv, vertx, dampx, damp16, vfull, mixer, factor,
-    wave32, trig, pair32, half32, xr, legm, mixed, lhs, part,
+    gv, legv, tab, sent, frecv, brecv, vertx, dampx, damp16, vfull, mixer, factor,
+    wave_ref, lon_ref, damp_ref, wave32, trig, pair32, half32, xr, legm, mixed, lhs, part,
     grid_sem, leg_sem, tab_sem, vsend_sem, vrecv_sem,
-    fsend_sem, frecv_sem, bsend_sem, brecv_sem, own_sem, part_sem,
+    fsend_sem, frecv_sem, bsend_sem, brecv_sem, own_sem, part_sem, small_sem,
 ):
     i = lax.axis_index("lat")
     j = lax.axis_index("lev")
@@ -72,6 +72,13 @@
     def landing(r):
         return brecv.at[r] if r < ROUNDS - 1 else last
 
+    small = [
+        pltpu.make_async_copy(wave_hbm, wave_ref, small_sem.at[0]),
+        pltpu.make_async_copy(lon_hbm, lon_ref, small_sem.at[1]),
+        pltpu.make_async_copy(damp_hbm, damp_ref, small_sem.at[2]),
+        pltpu.make_async_copy(vert_ref, vertx.at[j], small_sem.at[3]),
+    ]
+    small[0].start()
     for a in range(ROWS // CHUNK):
         grid_copy(a).start()
     barrier = pltpu.get_barrier_semaphore()
@@ -83,13 +90,6 @@
             device_id=(far_z[q // 32] + far_x[q // 8 % 4] + far_c[q // 4 % 2], far_y[q % 4]),
             device_id_type=MESH,
         )
-    for r in range(ROUNDS):
-        leg_copy(r).start()
-    damp16[...] = jnp.zeros_like(damp16)
-    damp16[:, 0:32] = jnp.broadcast_to(damp_ref[...].astype(F32).reshape(1, 32), (16, 32)).astype(
-        BF16
-    )
-
     def table(r):
         def spread(g, carry):
             wave32[pl.ds(g, 1), :] = jnp.full((1, 128), wave_ref[g * ROUNDS + r], jnp.int32)
@@ -111,6 +111,12 @@
         if r == ROUNDS - 1:
             tab_copy().start()
 
+    def by_row(r):
+        return sent.at[r].reshape(ROWS, PEERS, 2, LANES)
+
+    def by_level(r):
+        return sent.at[r].reshape(LEV, DEGREES, 2, LANES)
+
     def forward(r, first, count):
         def pair(p, carry):
             if r == 0:
@@ -121,8 +127,9 @@
 
             rows = gv.reshape(ROWS * LANES, LONS)[pl.ds(pl.multiple_of(p * 256, 256), 256), :]
             out = lax.dot_general(tab[r], rows, NT, preferred_element_type=F32).astype(BF16)
-            fsend.at[r, 2 * p].reshape(256, 128)[...] = out[:, 0:128]
-            fsend.at[r, 2 * p + 1].reshape(256, 128)[...] = out[:, 128:256]
+            for h in range(2):
+                place = sent.at[r, pl.ds((2 * p + h) * PEERS, PEERS)]
+                place.reshape(256, 128)[...] = out[:, h * 128 : (h + 1) * 128]
             return carry
 
         lax.fori_loop(first // 2, (first + count) // 2, pair, 0)
@@ -130,7 +137,7 @@
     def send_forward(r, first, count):
         def send(i2, j2):
             pltpu.make_async_remote_copy(
-                src_ref=fsend.at[r, pl.ds(first, count), i2 * LEV + j2],
+                src_ref=by_row(r).at[pl.ds(first, count), i2 * LEV + j2],
                 dst_ref=frecv.at[r, j, pl.ds(i * ROWS + first, count)],
                 send_sem=fsend_sem.at[r],
                 recv_sem=frecv_sem.at[r],
@@ -139,12 +146,12 @@
             ).start()
 
         to_partners(send)
-        frecv[r, j, pl.ds(i * ROWS + first, count)] = fsend[r, first : first + count, me]
+        frecv[r, j, pl.ds(i * ROWS + first, count)] = by_row(r)[first : first + count, me]
 
     def send_back(r):
         def send(i2, j2):
             pltpu.make_async_remote_copy(
-                src_ref=bsend.at[r, j2, pl.ds(i2 * ROWS, ROWS)],
+                src_ref=by_level(r).at[j2, pl.ds(i2 * ROWS, ROWS)],
                 dst_ref=landing(r).at[:, me],
                 send_sem=bsend_sem.at[r],
                 recv_sem=brecv_sem.at[r],
@@ -154,13 +161,13 @@
 
         to_partners(send)
         if r < ROUNDS - 1:
-            brecv[r, :, me] = bsend[r, j, pl.ds(i * ROWS, ROWS)]
+            brecv[r, :, me] = by_level(r)[j, pl.ds(i * ROWS, ROWS)]
         else:
             own_copy().start()
 
     def own_copy():
         return pltpu.make_async_copy(
-            bsend.at[ROUNDS - 1, j, pl.ds(i * ROWS, ROWS)], last.at[:, me], own_sem
+            by_level(ROUNDS - 1).at[j, pl.ds(i * ROWS, ROWS)], last.at[:, me], own_sem
         )
 
     def part_copy(s):
@@ -244,20 +251,29 @@
                     half32[pl.ds(h, 128, 2), :] = out[
                         :, h * 512 + p * 128 : h * 512 + (p + 1) * 128
                     ]
-                bsend.at[r, p].reshape(2 * DEGREES, 128)[s * 256 : (s + 1) * 256, :] = half32[
-                    ...
-                ].astype(BF16)
-
+                place = sent.at[r, pl.ds(p * DEGREES + s * 128, 128)]
+                place.reshape(256, 128)[...] = half32[...].astype(BF16)
+
+    small[0].wait()
     table(0)
-    forward(0, 0, 12)
+    forward(0, 0, 8)
     pl.semaphore_wait(barrier, PEERS - 1)
-    send_forward(0, 0, 12)
-    forward(0, 12, 8)
-    send_forward(0, 12, 8)
+    send_forward(0, 0, 8)
+    forward(0, 8, 12)
+    send_forward(0, 8, 12)
+    for copy in small[1:]:
+        copy.start()
+    for r in range(ROUNDS):
+        leg_copy(r).start()
+    for copy in small[1:]:
+        copy.wait()
+    damp16[...] = jnp.zeros_like(damp16)
+    damp16[:, 0:32] = jnp.broadcast_to(damp_ref[...].astype(F32).reshape(1, 32), (16, 32)).astype(
+        BF16
+    )
     for d in range(1, LEV):
         level_copy(vert_ref, vertx, 0, d).start()
         level_copy(damp16, dampx, 1, d).start()
-    vertx[j] = vert_ref[...]
     dampx[j] = damp16[...]
     for r in range(1, ROUNDS):
         table(r)
@@ -266,6 +282,7 @@
     build_mixer()
     for r in range(ROUNDS):
         leg_copy(r).wait()
+        wait_bytes(sent.at[r], r, fsend_sem)
         wait_bytes(frecv.at[r], r, frecv_sem)
         spectral(r)
         send_back(r)
@@ -288,8 +305,7 @@
         part_copy(s).wait()
     tab_copy().wait()
     for r in range(ROUNDS):
-        wait_bytes(fsend.at[r], r, fsend_sem)
-        wait_bytes(bsend.at[r], r, bsend_sem)
+        wait_bytes(sent.at[r], r, bsend_sem)
     own_copy().wait()
     wait_bytes(last, ROUNDS - 1, brecv_sem)
 
@@ -316,7 +332,6 @@
 
 def step(grid, legendre, vertical, damp, lon, waves):
     dma = pltpu.SemaphoreType.DMA
-    vmem = pl.BlockSpec(memory_space=pltpu.VMEM)
     any_spec = pl.BlockSpec(memory_space=pl.ANY)
     return pl.pallas_call(
         step_kernel,
@@ -325,14 +340,13 @@
             jax.ShapeDtypeStruct((ROWS * LANES, LONS), BF16),
             jax.ShapeDtypeStruct((256, LONS), BF16),
         ),
-        in_specs=[any_spec, any_spec, vmem, vmem, vmem, pl.BlockSpec(memory_space=pltpu.SMEM)],
+        in_specs=[pl.BlockSpec(memory_space=pltpu.HBM)] * 6,
         out_specs=(any_spec, any_spec, any_spec),
         scratch_shapes=[
             pltpu.VMEM((ROWS // CHUNK, CHUNK * LANES, LONS), BF16),
             pltpu.VMEM((ROUNDS, DEGREES, DEGREES), BF16),
             pltpu.VMEM((ROUNDS, 256, LONS), BF16),
-            pltpu.VMEM((ROUNDS, ROWS, PEERS, 2, LANES), BF16),
-            pltpu.VMEM((ROUNDS, LEV, DEGREES, 2, LANES), BF16),
+            pltpu.VMEM((ROUNDS, ROWS * PEERS, 2, LANES), BF16),
             pltpu.VMEM((ROUNDS, LEV, DEGREES, 2, LANES), BF16),
             pltpu.VMEM((ROUNDS - 1, ROWS, PEERS, 2, LANES), BF16),
             pltpu.VMEM((LEV, 32, 128), BF16),
@@ -341,6 +355,9 @@
             pltpu.VMEM((128, 128), BF16),
             pltpu.VMEM((512, 512), BF16),
             pltpu.VMEM((DEGREES, 512), F32),
+            pltpu.SMEM((DEGREES,), jnp.int32),
+            pltpu.VMEM((DEGREES,), jnp.int32),
+            pltpu.VMEM((32,), BF16),
             pltpu.VMEM((PEERS, 128), jnp.int32),
             pltpu.VMEM((2, PEERS, 128), F32),
             pltpu.VMEM((2 * DEGREES, 128), F32),
@@ -351,15 +368,15 @@
             pltpu.VMEM((CHUNK * 128, (ROUNDS - 1) * 256), BF16),
             pltpu.VMEM((2, CHUNK * 128, LONS), BF16),
             dma((ROWS // CHUNK,)), dma((ROUNDS,)), dma, dma((2,)), dma((2,)),
-            dma((ROUNDS,)), dma((ROUNDS,)), dma((ROUNDS,)), dma((ROUNDS,)), dma, dma((2,)),
+            dma((ROUNDS,)), dma((ROUNDS,)), dma((ROUNDS,)), dma((ROUNDS,)), dma, dma((2,)), dma((4,)),
         ],
         compiler_params=pltpu.CompilerParams(
-            collective_id=0, has_side_effects=True, vmem_limit_bytes=62 * 2**20
+            collective_id=0, has_side_effects=True, vmem_limit_bytes=67043328
         ),
     )(grid, legendre, vertical, damp, lon, waves)
 
 
-def finish_kernel(last_ref, tab_ref, part_ref, out_ref, lhs, stage, sem):
+def finish_kernel(last_ref, tab_ref, part_ref, out_ref, stage, sem):
     s = pl.program_id(0)
     slot = s % 2
 
@@ -370,15 +387,15 @@
             sem.at[where],
         )
 
-    for a in range(PIECE):
-        lhs[a * 128 : (a + 1) * 128, :] = last_ref.at[a].reshape(256, 128)[...].T
-
     @pl.when(s >= 2)
     def _():
         out_copy(s - 2, slot).wait()
 
-    out = jnp.dot(lhs[...], tab_ref[...], preferred_element_type=F32)
-    stage[slot] = (out + part_ref[...].astype(F32)).astype(BF16)
+    for a in range(PIECE):
+        block = last_ref.at[a].reshape(256, 128)[...]
+        out = lax.dot_general(block, tab_ref[...], TN, preferred_element_type=F32)
+        rows = slice(a * 128, (a + 1) * 128)
+        stage[slot, rows, :] = (out + part_ref[rows, :].astype(F32)).astype(BF16)
     out_copy(s, slot).start()
 
     @pl.when(s == pl.num_programs(0) - 1)
@@ -399,7 +416,6 @@
         ],
         out_specs=pl.BlockSpec(memory_space=pl.ANY),
         scratch_shapes=[
-            pltpu.VMEM((PIECE * 128, 256), BF16),
             pltpu.VMEM((2, PIECE * 128, LONS), BF16),
             pltpu.SemaphoreType.DMA((2,)),
         ],

time: 163 us -> 163 us (level)
  Pallas kernels: 163 us -> 161 us
where the time goes in v2:
time: 163 us; the launch traced here: 162 us
  Pallas kernels  161 us (99%)
    pallas_call x1, Pallas kernels, step(): pl.pallas_call(step_kernel, out_shape=(jax.ShapeDtypeStruct((ROWS, PEERS,...  155 us
    pallas_call x1, Pallas kernels, finish(): pl.pallas_call(finish_kernel, grid=(ROWS // PIECE,), out_shape=jax.ShapeD...  6.43 us

profile of v2, /device:TPU:1, one launch (start us, length us, event | category | flops | bytes accessed | tf_op | source)
XLA Modules:
  0.0 161.5 jit_solution(9508954269768852777)
XLA Ops:
  0.0 154.9 %shard_map.64 = (bf16[20,128,2,128]{3,2,1,0:T(2,128)(2,1)}, bf16[2560,1280]{1,0:T(8,128)(2,1)}, bf16[256,1280]{1,0:T(8,128)(2,1)}) custom-call(bf16[20,32,4,1280]{3,2,1,0:T(4,128)(2,1)} %grid_ref.1, bf16[20,640,640]{2,1,0:T(8,128)(2,1)} %leg_ref.1, bf16[32,128]{1,0:T(8,128)(2,1)} %vert_ref.1, bf16[32]{0:T(256)(128)(2,1)} %damp_hbm.1, s32[640]{0:T(1024)} %lon_hbm.1, ...), custom_call_target="tpu_custom_call" | custom-call | tf_op jit(solution)/shard_map/pallas_call | solution.py:336
  154.9 6.4 %shard_map.65 = bf16[20,32,4,1280]{3,2,1,0:T(4,128)(2,1)} custom-call(bf16[20,128,2,128]{3,2,1,0:T(2,128)(2,1)} %get-tuple-element.8.last_ref, bf16[256,1280]{1,0:T(8,128)(2,1)} %get-tuple-element.9.tab_ref, bf16[2560,1280]{1,0:T(8,128)(2,1)} %get-tuple-element.10.part_ref), custom_call_target="tpu_custom_call" | custom-call | tf_op jit(solution)/shard_map/pallas_call | solution.py:408

commit v3 on v2

--- a/solution.py
+++ b/solution.py
@@ -72,6 +72,14 @@
     def landing(r):
         return brecv.at[r] if r < ROUNDS - 1 else last
 
+    barrier = pltpu.get_barrier_semaphore()
+    for q in sorted(range(1, PEERS), key=hops, reverse=True):
+        pl.semaphore_signal(
+            barrier,
+            inc=1,
+            device_id=(far_z[q // 32] + far_x[q // 8 % 4] + far_c[q // 4 % 2], far_y[q % 4]),
+            device_id_type=MESH,
+        )
     small = [
         pltpu.make_async_copy(wave_hbm, wave_ref, small_sem.at[0]),
         pltpu.make_async_copy(lon_hbm, lon_ref, small_sem.at[1]),
@@ -81,15 +89,6 @@
     small[0].start()
     for a in range(ROWS // CHUNK):
         grid_copy(a).start()
-    barrier = pltpu.get_barrier_semaphore()
-    for k in range(1, PEERS):
-        q = (k * 45) % PEERS
-        pl.semaphore_signal(
-            barrier,
-            inc=1,
-            device_id=(far_z[q // 32] + far_x[q // 8 % 4] + far_c[q // 4 % 2], far_y[q % 4]),
-            device_id_type=MESH,
-        )
     def table(r):
         def spread(g, carry):
             wave32[pl.ds(g, 1), :] = jnp.full((1, 128), wave_ref[g * ROUNDS + r], jnp.int32)
@@ -310,6 +309,10 @@
     wait_bytes(last, ROUNDS - 1, brecv_sem)
 
 
+def hops(q):
+    return sum(min(d, 4 - d) for d in (q // 32, q // 8 % 4, q % 4))
+
+
 def unit_circle(steps):
     turns = jnp.floor(steps * (1.0 / LONS))
     rest = steps - turns * LONS

time: 163 us -> 161 us (0.988); the launches traced: 162 us -> 161 us
  no operation moved by 1% of the time
where the time goes in v3:
time: 161 us
  Pallas kernels  161 us (100%)
    pallas_call x1, Pallas kernels, step(): pl.pallas_call(step_kernel, out_shape=(jax.ShapeDtypeStruct((ROWS, PEERS,...  155 us
    pallas_call x1, Pallas kernels, finish(): pl.pallas_call(finish_kernel, grid=(ROWS // PIECE,), out_shape=jax.ShapeD...  6.43 us

profile of v3, /device:TPU:1, one launch (start us, length us, event | category | flops | bytes accessed | tf_op | source)
XLA Modules:
  0.0 161.3 jit_solution(14473707069287303779)
XLA Ops:
  0.0 154.7 %shard_map.64 = (bf16[20,128,2,128]{3,2,1,0:T(2,128)(2,1)}, bf16[2560,1280]{1,0:T(8,128)(2,1)}, bf16[256,1280]{1,0:T(8,128)(2,1)}) custom-call(bf16[20,32,4,1280]{3,2,1,0:T(4,128)(2,1)} %grid_ref.1, bf16[20,640,640]{2,1,0:T(8,128)(2,1)} %leg_ref.1, bf16[32,128]{1,0:T(8,128)(2,1)} %vert_ref.1, bf16[32]{0:T(256)(128)(2,1)} %damp_hbm.1, s32[640]{0:T(1024)} %lon_hbm.1, ...), custom_call_target="tpu_custom_call" | custom-call | tf_op jit(solution)/shard_map/pallas_call | solution.py:339
  154.7 6.4 %shard_map.65 = bf16[20,32,4,1280]{3,2,1,0:T(4,128)(2,1)} custom-call(bf16[20,128,2,128]{3,2,1,0:T(2,128)(2,1)} %get-tuple-element.8.last_ref, bf16[256,1280]{1,0:T(8,128)(2,1)} %get-tuple-element.9.tab_ref, bf16[2560,1280]{1,0:T(8,128)(2,1)} %get-tuple-element.10.part_ref), custom_call_target="tpu_custom_call" | custom-call | tf_op jit(solution)/shard_map/pallas_call | solution.py:411
